TPU v7x, 32 devices: a whole 2x2x4 slice. The times are simulated.
32 devices in a mesh: gx: 4 (over y, x), gy: 2 (over core), gz: 4 (over z).
Axes of the slice: x: 2, y: 2, z: 4, core: 2. Of those that a mesh axis runs over, the one named last changes fastest.
Arguments:
- spectrum: float32 [3, 2, 16, 16, 2048], P(None, None, ('gy', 'gx'), None, 'gz'), may hold values from -0.3125 to 0.3125
- theta: float32 [16, 16, 8192], P('gy', 'gz', 'gx'), may hold values from -6 to 6
- section_sum: float32 [16, 16, 8192], P('gy', 'gz', 'gx'), may hold values from -6 to 6
- seg_offset: int32 [4], replicated, may hold values from 0 to 2560, as said below
- seg_length: int32 [4], replicated, may hold values from 512 to 1536, as said below
- stencil_index: int32 [8, 8192], replicated, may hold values from 0 to 1535, as said below
- stencil_weight: float32 [8, 8192], replicated, may hold values from 0 to 0.25
Outputs:
- theta_next: float32 [16, 16, 8192], P('gy', 'gz', 'gx')
- section_next: float32 [16, 16, 8192], P('gy', 'gz', 'gx')
Inputs may be any that keep to these rules, and one draw needn't show every extreme that they name: `seg_length`: some block's segment holds exactly 1536 cells. For every block i, seg_offset[i] + 1536 <= 4096. `stencil_index`: positions count from the start of the segment of the scalar cell's x block; taps at or past that segment's length are padding.
All inputs are finite; a program needn't handle non-finite values.
Results may differ from a plain program's by a relative error of at most 0.00005.
Values sent between devices are 32-bit elements; how exact they have to be, the bound alone decides.
A program may use at most 64 MiB of HBM per device.

v0:
```python
import math

import jax
import jax.numpy as jnp
from jax import lax
from jax.sharding import PartitionSpec as P

first_coeffs = (0.8, -0.2, 4.0 / 105.0, -1.0 / 280.0)
second_coeffs = (1.6, -0.2, 8.0 / 315.0, -1.0 / 560.0)
center_coeff = -205.0 / 72.0
diffusivity = 0.15
time_step = 0.4
section_keep = -5.0 / 9.0
section_gain = 15.0 / 16.0


def extended(cells, sides, width):
    for axis, dim in sides:
        count = lax.axis_size(axis)
        head = lax.slice_in_dim(cells, 0, width, axis=dim)
        tail = lax.slice_in_dim(cells, cells.shape[dim] - width, cells.shape[dim], axis=dim)
        cells = jnp.concatenate(
            [
                lax.ppermute(tail, axis, [(i, (i + 1) % count) for i in range(count)]),
                cells,
                lax.ppermute(head, axis, [((i + 1) % count, i) for i in range(count)]),
            ],
            axis=dim,
        )
    return cells


def contract(pattern, first_term, second_term):
    return jnp.einsum(pattern, first_term, second_term, precision=lax.Precision.HIGHEST)


def phase_table(rows_index, cols_index, period):
    wound = rows_index[:, None] * cols_index[None, :] % period
    angle = 2.0 * math.pi / period * wound.astype(jnp.float32)
    return (jnp.cos(angle), jnp.sin(angle))


def inverse_lines(spectrum):
    mode_count = spectrum.shape[-1]
    length = 2 * mode_count
    factor = math.isqrt(length)
    line_shape = (3,) + spectrum.shape[2:4] + (factor // 2, factor)
    real_part = spectrum[:, 0].reshape(line_shape)
    imag_part = spectrum[:, 1].reshape(line_shape)
    outer_index = jnp.arange(factor // 2, dtype=jnp.int32)
    inner_index = jnp.arange(factor, dtype=jnp.int32)
    cosine_first, sine_first = phase_table(outer_index, inner_index, factor)
    first_real = contract("cyzak,aj->cyzjk", real_part, cosine_first) - contract(
        "cyzak,aj->cyzjk", imag_part, sine_first
    )
    first_imag = contract("cyzak,aj->cyzjk", real_part, sine_first) + contract(
        "cyzak,aj->cyzjk", imag_part, cosine_first
    )
    cosine_twist, sine_twist = phase_table(inner_index, inner_index, length)
    twist_real = first_real * cosine_twist - first_imag * sine_twist
    twist_imag = first_real * sine_twist + first_imag * cosine_twist
    cosine_last, sine_last = phase_table(inner_index, inner_index, factor)
    physical = contract("cyzjk,km->cyzmj", twist_real, cosine_last) - contract(
        "cyzjk,km->cyzmj", twist_imag, sine_last
    )
    return physical.reshape((3,) + spectrum.shape[2:4] + (length,))


def pick_entry(table, entry):
    return jnp.sum(jnp.where(jnp.arange(table.shape[0], dtype=jnp.int32) == entry, table, 0))


def interpolate(segment, taps_index, taps_weight, live_count):
    live_weight = jnp.where(taps_index < live_count, taps_weight, 0.0)
    position = jnp.arange(segment.shape[-1], dtype=jnp.int32)
    matrix = jnp.zeros((segment.shape[-1], taps_index.shape[1]), jnp.float32)
    for tap_number in range(taps_index.shape[0]):
        matrix = matrix + jnp.where(
            position[:, None] == taps_index[tap_number][None, :],
            live_weight[tap_number][None, :],
            0.0,
        )
    return contract("cyzm,ms->cyzs", segment, matrix)


def body(spectrum, theta, section_sum, seg_offset, seg_length, stencil_index, stencil_weight):
    blocks = lax.axis_size("gx")
    columns = lax.all_to_all(spectrum, "gz", split_axis=3, concat_axis=4, tiled=True)
    velocity = inverse_lines(columns)
    line_length = velocity.shape[-1]
    widest = 3 * line_length // (2 * blocks)
    block_cells = stencil_index.shape[1] // blocks
    block_numbers = jnp.arange(blocks, dtype=jnp.int32)

    def block_tables(block_number):
        taps_index = lax.dynamic_slice_in_dim(
            stencil_index, block_number * block_cells, block_cells, 1
        )
        taps_weight = lax.dynamic_slice_in_dim(
            stencil_weight, block_number * block_cells, block_cells, 1
        )
        return (
            taps_index,
            taps_weight,
            pick_entry(seg_offset, block_number),
            pick_entry(seg_length, block_number),
        )

    def sample(block_number):
        taps_index, taps_weight, seg_start, live_count = block_tables(block_number)
        segment = lax.dynamic_slice_in_dim(velocity, seg_start, widest, 3)
        return interpolate(segment, taps_index, taps_weight, live_count)

    pieces = lax.map(sample, block_numbers)
    carried = lax.all_to_all(pieces, "gx", split_axis=0, concat_axis=2, tiled=True)[0]
    padded = extended(theta, (("gx", 2), ("gy", 0), ("gz", 1)), 4)
    rows_count, depth, cells = theta.shape

    def window(along_y, along_z, along_x):
        return padded[
            4 + along_y : 4 + along_y + rows_count,
            4 + along_z : 4 + along_z + depth,
            4 + along_x : 4 + along_x + cells,
        ]

    grad_x = jnp.zeros_like(theta)
    grad_y = jnp.zeros_like(theta)
    grad_z = jnp.zeros_like(theta)
    laplace = 3.0 * center_coeff * theta
    for reach in range(1, 5):
        ahead_x = window(0, 0, reach)
        behind_x = window(0, 0, -reach)
        ahead_y = window(reach, 0, 0)
        behind_y = window(-reach, 0, 0)
        ahead_z = window(0, reach, 0)
        behind_z = window(0, -reach, 0)
        first = first_coeffs[reach - 1]
        second = second_coeffs[reach - 1]
        grad_x = grad_x + first * (ahead_x - behind_x)
        grad_y = grad_y + first * (ahead_y - behind_y)
        grad_z = grad_z + first * (ahead_z - behind_z)
        laplace = laplace + second * (ahead_x + behind_x + ahead_y + behind_y + ahead_z + behind_z)
    change = (
        -(carried[0] * grad_x + carried[1] * grad_y + carried[2] * grad_z) + diffusivity * laplace
    )
    section_next = section_keep * section_sum + time_step * change
    theta_next = theta + section_gain * section_next
    return (theta_next, section_next)


def solution(mesh):
    placed = (
        P(None, None, ("gy", "gx"), None, "gz"),
        P("gy", "gz", "gx"),
        P("gy", "gz", "gx"),
        P(),
        P(),
        P(),
        P(),
    )
    return jax.shard_map(
        body,
        mesh=mesh,
        in_specs=placed,
        out_specs=(P("gy", "gz", "gx"), P("gy", "gz", "gx")),
        check_vma=False,
    )
```

profile of v0, /device:TPU:0, one launch (start us, length us, event | category | flops | bytes accessed | tf_op | source)
XLA Modules:
  0.0 177.1 jit_solution(10833433747002345924)
XLA Ops:
  0.6 0.0 copy-start
  0.6 2.1 %copy.16 = f32[3,2,2,16,512]{4,0,2,1,3:T(4,128)} copy(f32[3,2,2,16,512]{4,3,2,1,0:T(8,128)} %param.9) | data formatting | bytes 786432 | tf_op args[0]
  2.8 6.3 %all-to-all-start = ((f32[3,2,2,16,512]{4,0,2,1,3:T(4,128)}), f32[3,2,2,16,512]{4,0,2,1,3:T(4,128)S(1)}, u32[]{:S(2)}, u32[]{:S(2)}) async-start(f32[3,2,2,16,512]{4,0,2,1,3:T(4,128)} %copy.16), calls=%async_computation | async-start | bytes 1048576 | tf_op jit(solution)/shard_map/all_to_all | solution.py:88
  9.1 0.0 copy-done
  9.1 0.1 fusion.140
  9.2 2.4 %collective-permute-start = (f32[8,4,4]{2,1,0:T(4,128)S(1)}, f32[8,4,4]{2,1,0:T(4,128)S(1)}, u32[]{:S(2)}, u32[]{:S(2)}) collective-permute-start(f32[8,4,4]{2,1,0:T(4,128)S(1)} %get-tuple-element.88), channel_id=1, source_target_pairs={{8,0},{16,8},{24,16},{0,24},{9,1},{17,9},{25,17},{1,25},{10,2},{18... | collective-permute-start | bytes 1544 | tf_op jit(solution)/shard_map/ppermute | solution.py:26
  11.6 0.0 collective-permute-start.1
  11.6 0.1 fusion.101
  11.8 0.1 fusion.100
  11.9 0.1 copy.18
  12.0 0.1 copy.19
  12.1 1.0 collective-permute-done
  13.1 3.2 %collective-permute-done.1 = f32[8,4,4]{2,1,0:T(4,128)S(1)} collective-permute-done((f32[8,4,4]{2,1,0:T(4,128)S(1)}, f32[8,4,4]{2,1,0:T(4,128)S(1)}, u32[]{:S(2)}, u32[]{:S(2)}) %collective-permute-start.1) | collective-permute-done | bytes 544 | tf_op jit(solution)/shard_map/ppermute | solution.py:24
  16.3 0.3 concatenate.43
  16.6 0.1 collective-permute-start.2
  16.7 0.5 collective-permute-start.3
  17.2 6.4 %all-to-all-done = f32[3,2,2,16,512]{4,0,2,1,3:T(4,128)S(1)} async-done(((f32[3,2,2,16,512]{4,0,2,1,3:T(4,128)}), f32[3,2,2,16,512]{4,0,2,1,3:T(4,128)S(1)}, u32[]{:S(2)}, u32[]{:S(2)}) %all-to-all-start) | async-done | bytes 393248 | tf_op jit(solution)/shard_map/all_to_all | solution.py:88
  23.6 0.3 copy.17
  23.9 0.3 all_to_all.27
  24.2 0.2 reshape_squeeze.6
  24.5 0.9 fusion.95
  25.4 0.9 fusion.93
  26.3 0.2 reshape_squeeze.7
  26.5 0.9 convolution_add_fusion
  27.4 0.9 convolution_subtract_fusion.1
  28.3 2.5 %fusion.47 = f32[64,3,2,4,64]{4,0,3,2,1:T(8,128)S(1)} fusion(f32[64,3,2,4,64]{4,0,3,2,1:T(8,128)S(1)} %convolution_add_fusion, f32[64,3,2,4,64]{4,0,3,2,1:T(8,128)S(1)} %convolution_subtract_fusion.1, f32[64,64]{1,0:T(8,128)S(1)} %copy.19, f32[64,64]{1,0:T(8,128)S(1)} %copy.18), kind=kOutput, calls=%fused_computation.59 | convolution fusion | flops 75849728 | bytes 1212416 | tf_op jit(solution)/shard_map/cyzjk,km->cyzmj/dot_general | solution.py:34
  30.8 2.5 %fusion.45 = f32[3,2,4,64,64]{4,3,2,1,0:T(8,128)S(1)} fusion(f32[64,3,2,4,64]{4,0,3,2,1:T(8,128)S(1)} %fusion.47, f32[64,3,2,4,64]{4,0,3,2,1:T(8,128)S(1)} %convolution_add_fusion, f32[64,3,2,4,64]{4,0,3,2,1:T(8,128)S(1)} %convolution_subtract_fusion.1, f32[64,64]{1,0:T(8,128)S(1)} %copy.19, f32[64,64]{1,0:T(8,128)S(1)} %copy.18), kind=kOutput, calls=%fused_computation.55 | convolution fusion | flops 75948032 | bytes 1605632 | tf_op jit(solution)/shard_map/cyzjk,km->cyzmj/dot_general | solution.py:34
  33.3 0.0 copy-start.3
  33.3 0.0 copy-start.4
  33.3 0.3 reshape.50
  33.6 0.6 copy-done.1
  34.2 0.0 copy-done.3
  34.2 106.4 %while.10 = (s32[]{:T(128)}, f32[4,3,2,4,2048]{4,3,2,1,0:T(4,128)}, s32[4]{0:T(128)S(1)}, s32[4]{0:T(128)S(1)}, f32[3,2,4,4096]{3,2,1,0:T(4,128)S(1)}, /*index=5...) while((s32[]{:T(128)}, f32[4,3,2,4,2048]{4,3,2,1,0:T(4,128)}, ...), condition=%wide.region_3.4_spmd, body=%wide.region_0.3_spmd.sunk | while | flops 978354240 | bytes 934845 | solution.py:114
  34.2 0.6 dynamic_slice.26
  35.5 1.3 fusion.152
  36.8 1.5 dynamic-slice_select_fusion.2
  38.4 0.2 constant_dynamic-slice_fusion.2
  40.5 20.4 %fusion.154 = f32[4,3,2,4,2048]{4,3,2,1,0:T(4,128)} fusion(f32[4,3,2,4,2048]{4,3,2,1,0:T(4,128)} %get-tuple-element.196, s32[]{:T(128)} %get-tuple-element.195, f32[2048]{0:T(1024)S(1)} %bitcast.146, s32[2048]{0:T(1024)S(1)} %bitcast.154, f32[2048]{0:T(1024)S(1)} %bitcast.147, s32[2048]{0:T(1024)S(1)} %bitcast.155, f32[2048]{0:T(1024)S(1)} %bitcast.148, ...), kind=kOutput, calls=%fused_computation.43.clone.1 | convolution fusion | flops 978321408 | bytes 475652 | tf_op jit(solution)/shard_map/while/body/eval_jaxpr/cyzm,ms->cyzs/dot_general | solution.py:34
  60.8 0.6 dynamic_slice.26
  62.1 1.3 fusion.152
  63.4 1.5 dynamic-slice_select_fusion.2
  64.9 0.2 constant_dynamic-slice_fusion.2
  67.1 20.4 %fusion.154 = f32[4,3,2,4,2048]{4,3,2,1,0:T(4,128)} fusion(f32[4,3,2,4,2048]{4,3,2,1,0:T(4,128)} %get-tuple-element.196, s32[]{:T(128)} %get-tuple-element.195, f32[2048]{0:T(1024)S(1)} %bitcast.146, s32[2048]{0:T(1024)S(1)} %bitcast.154, f32[2048]{0:T(1024)S(1)} %bitcast.147, s32[2048]{0:T(1024)S(1)} %bitcast.155, f32[2048]{0:T(1024)S(1)} %bitcast.148, ...), kind=kOutput, calls=%fused_computation.43.clone.1 | convolution fusion | flops 978321408 | bytes 475652 | tf_op jit(solution)/shard_map/while/body/eval_jaxpr/cyzm,ms->cyzs/dot_general | solution.py:34
  87.4 0.6 dynamic_slice.26
  88.7 1.3 fusion.152
  90.0 1.5 dynamic-slice_select_fusion.2
  91.5 0.2 constant_dynamic-slice_fusion.2
  93.7 20.4 %fusion.154 = f32[4,3,2,4,2048]{4,3,2,1,0:T(4,128)} fusion(f32[4,3,2,4,2048]{4,3,2,1,0:T(4,128)} %get-tuple-element.196, s32[]{:T(128)} %get-tuple-element.195, f32[2048]{0:T(1024)S(1)} %bitcast.146, s32[2048]{0:T(1024)S(1)} %bitcast.154, f32[2048]{0:T(1024)S(1)} %bitcast.147, s32[2048]{0:T(1024)S(1)} %bitcast.155, f32[2048]{0:T(1024)S(1)} %bitcast.148, ...), kind=kOutput, calls=%fused_computation.43.clone.1 | convolution fusion | flops 978321408 | bytes 475652 | tf_op jit(solution)/shard_map/while/body/eval_jaxpr/cyzm,ms->cyzs/dot_general | solution.py:34
  114.0 0.6 dynamic_slice.26
  115.3 1.3 fusion.152
  116.6 1.5 dynamic-slice_select_fusion.2
  118.1 0.2 constant_dynamic-slice_fusion.2
  120.2 20.4 %fusion.154 = f32[4,3,2,4,2048]{4,3,2,1,0:T(4,128)} fusion(f32[4,3,2,4,2048]{4,3,2,1,0:T(4,128)} %get-tuple-element.196, s32[]{:T(128)} %get-tuple-element.195, f32[2048]{0:T(1024)S(1)} %bitcast.146, s32[2048]{0:T(1024)S(1)} %bitcast.154, f32[2048]{0:T(1024)S(1)} %bitcast.147, s32[2048]{0:T(1024)S(1)} %bitcast.155, f32[2048]{0:T(1024)S(1)} %bitcast.148, ...), kind=kOutput, calls=%fused_computation.43.clone.1 | convolution fusion | flops 978321408 | bytes 475652 | tf_op jit(solution)/shard_map/while/body/eval_jaxpr/cyzm,ms->cyzs/dot_general | solution.py:34
  140.6 3.7 %all-to-all-start.1 = ((f32[4,3,2,4,2048]{4,3,2,1,0:T(4,128)}), f32[4,3,2,4,2048]{4,3,2,1,0:T(4,128)S(1)}, u32[]{:S(2)}, u32[]{:S(2)}) async-start(f32[4,3,2,4,2048]{4,3,2,1,0:T(4,128)} %get-tuple-element.44), calls=%async_computation.1 | async-start | bytes 1572864 | tf_op jit(solution)/shard_map/all_to_all | solution.py:115
  144.4 0.0 collective-permute-done.2
  144.4 0.0 collective-permute-done.3
  144.4 0.9 pad_maximum_fusion
  145.3 1.5 collective-permute-start.4
  146.8 0.6 collective-permute-start.5
  147.4 7.3 %all-to-all-done.1 = f32[4,3,2,4,2048]{4,3,2,1,0:T(4,128)S(1)} async-done(((f32[4,3,2,4,2048]{4,3,2,1,0:T(4,128)}), f32[4,3,2,4,2048]{4,3,2,1,0:T(4,128)S(1)}, u32[]{:S(2)}, u32[]{:S(2)}) %all-to-all-start.1) | async-done | bytes 786464 | tf_op jit(solution)/shard_map/all_to_all | solution.py:115
  154.7 0.1 fusion.137
  154.7 16.4 %collective-permute-done.4 = f32[16,4,2056]{2,1,0:T(4,128)S(1)} collective-permute-done((f32[16,4,2056]{2,1,0:T(4,128)}, f32[16,4,2056]{2,1,0:T(4,128)S(1)}, u32[]{:S(2)}, u32[]{:S(2)}) %collective-permute-start.4) | collective-permute-done | bytes 526368 | tf_op jit(solution)/shard_map/ppermute | solution.py:26
  171.1 0.0 collective-permute-done.5
  171.1 6.0 %multiply_add_fusion = (f32[8,4,2048]{2,1,0:T(4,128)}, f32[8,4,2048]{2,1,0:T(4,128)}) fusion(f32[8,4,2048]{2,1,0:T(4,128)S(1)} %copy-done, f32[16,4,2056]{2,1,0:T(4,128)S(1)} %collective-permute-done.5, f32[16,4,2056]{2,1,0:T(4,128)S(1)} %collective-permute-done.4, f32[4,4,2056]{2,1,0:T(4,128)S(1)} %collective-permute-done.2, ...), kind=kLoop, calls=%fused_computation.118 | loop fusion | flops 6881280 | bytes 5095424 | tf_op jit(solution)/shard_map/add | solution.py:147
  (14 shorter events, 0.3 us)
Async XLA Ops:
  0.6 8.5 %copy-start = (f32[8,4,2048]{2,1,0:T(4,128)S(1)}, f32[8,4,2048]{2,1,0:T(4,128)}, u32[]{:S(2)}) copy-start(f32[8,4,2048]{2,1,0:T(4,128)} %param.10) | copy-start | bytes 786436
  2.8 20.8 %all-to-all-start = ((f32[3,2,2,16,512]{4,0,2,1,3:T(4,128)}), f32[3,2,2,16,512]{4,0,2,1,3:T(4,128)S(1)}, u32[]{:S(2)}, u32[]{:S(2)}) async-start(f32[3,2,2,16,512]{4,0,2,1,3:T(4,128)} %copy.16), calls=%async_computation | async-start | bytes 1048576 | tf_op jit(solution)/shard_map/all_to_all | solution.py:88
  9.2 3.9 %collective-permute-start = (f32[8,4,4]{2,1,0:T(4,128)S(1)}, f32[8,4,4]{2,1,0:T(4,128)S(1)}, u32[]{:S(2)}, u32[]{:S(2)}) collective-permute-start(f32[8,4,4]{2,1,0:T(4,128)S(1)} %get-tuple-element.88), channel_id=1, source_target_pairs={{8,0},{16,8},{24,16},{0,24},{9,1},{17,9},{25,17},{1,25},{10,2},{18... | collective-permute-start | bytes 1544 | tf_op jit(solution)/shard_map/ppermute | solution.py:26
  11.6 4.6 %collective-permute-start.1 = (f32[8,4,4]{2,1,0:T(4,128)S(1)}, f32[8,4,4]{2,1,0:T(4,128)S(1)}, u32[]{:S(2)}, u32[]{:S(2)}) collective-permute-start(f32[8,4,4]{2,1,0:T(4,128)S(1)} %get-tuple-element.89), channel_id=1, source_target_pairs={{0,8},{8,16},{16,24},{24,0},{1,9},{9,17},{17,25},{25,1},{2,10},{10... | collective-permute-start | bytes 1544 | tf_op jit(solution)/shard_map/ppermute | solution.py:24
  16.6 127.7 %collective-permute-start.2 = (f32[4,4,2056]{2,1,0:T(4,128)S(1)}, f32[4,4,2056]{2,1,0:T(4,128)S(1)}, u32[]{:S(2)}, u32[]{:S(2)}) collective-permute-start(f32[4,4,2056]{2,1,0:T(4,128)S(1)} %get-tuple-element.87), channel_id=1, source_target_pairs={{4,0},{0,4},{5,1},{1,5},{6,2},{2,6},{7,3},{3,7},{12,8},{8,12},{13,... | collective-permute-start | bytes 394760 | tf_op jit(solution)/shard_map/ppermute | solution.py:26
  16.7 127.7 %collective-permute-start.3 = (f32[4,4,2056]{2,1,0:T(4,128)S(1)}, f32[4,4,2056]{2,1,0:T(4,128)S(1)}, u32[]{:S(2)}, u32[]{:S(2)}) collective-permute-start(f32[4,4,2056]{2,1,0:T(4,128)S(1)} %get-tuple-element.86), channel_id=1, source_target_pairs={{0,4},{4,0},{1,5},{5,1},{2,6},{6,2},{3,7},{7,3},{8,12},{12,8},{9,1... | collective-permute-start | bytes 394760 | tf_op jit(solution)/shard_map/ppermute | solution.py:24
  33.3 1.0 copy-start.1
  33.3 0.9 copy-start.3
  33.3 0.9 copy-start.4
  140.6 14.0 %all-to-all-start.1 = ((f32[4,3,2,4,2048]{4,3,2,1,0:T(4,128)}), f32[4,3,2,4,2048]{4,3,2,1,0:T(4,128)S(1)}, u32[]{:S(2)}, u32[]{:S(2)}) async-start(f32[4,3,2,4,2048]{4,3,2,1,0:T(4,128)} %get-tuple-element.44), calls=%async_computation.1 | async-start | bytes 1572864 | tf_op jit(solution)/shard_map/all_to_all | solution.py:115
  145.3 25.8 %collective-permute-start.4 = (f32[16,4,2056]{2,1,0:T(4,128)}, f32[16,4,2056]{2,1,0:T(4,128)S(1)}, u32[]{:S(2)}, u32[]{:S(2)}) collective-permute-start(f32[16,4,2056]{2,1,0:T(4,128)} %pad_maximum_fusion), channel_id=1, source_target_pairs={{1,0},{2,1},{3,2},{0,3},{5,4},{6,5},{7,6},{4,7},{9,8},{10,9},{11,1... | collective-permute-start | bytes 1579016 | tf_op jit(solution)/shard_map/ppermute | solution.py:26
  146.8 24.3 %collective-permute-start.5 = (f32[16,4,2056]{2,1,0:T(4,128)}, f32[16,4,2056]{2,1,0:T(4,128)S(1)}, u32[]{:S(2)}, u32[]{:S(2)}) collective-permute-start(f32[16,4,2056]{2,1,0:T(4,128)} %pad_maximum_fusion), channel_id=1, source_target_pairs={{0,1},{1,2},{2,3},{3,0},{4,5},{5,6},{6,7},{7,4},{8,9},{9,10},{10,1... | collective-permute-start | bytes 1579016 | tf_op jit(solution)/shard_map/ppermute | solution.py:24
  154.7 16.4 %copy-start.2 = (f32[8,4,2048]{2,1,0:T(4,128)S(1)}, f32[8,4,2048]{2,1,0:T(4,128)}, u32[]{:S(2)}) copy-start(f32[8,4,2048]{2,1,0:T(4,128)} %param.11) | copy-start | bytes 786436
where the time goes:
time: 178 us; the launch traced here: 177 us
  matrix products  90.1 us (51%)
  waiting for transfers between devices  34.2 us (19%)
  other arithmetic  18.5 us (10%)
  starting transfers between devices  15.1 us (8%)
  loops' own time  10.3 us (6%)
  local copies, waits for them, and re-layouts  8.11 us (5%)
    dot_general x10, matrix products, contract(): jnp.einsum(pattern, first_term, second_term, precision=lax.Precision.HIGH...  90.1 us
    ppermute x3, waiting for transfers between devices, extended(): lax.ppermute(head, axis, [((i + 1) % count, i) for i in range(count)])  17.4 us
    another operation x1, loops' own time, body(): pieces = lax.map(sample, block_numbers)  10.3 us
    all_to_all x1, waiting for transfers between devices, body(): lax.all_to_all(pieces, 'gx', split_axis=0, concat_axis=2, tiled=True)[0]  7.29 us
    all_to_all x1, waiting for transfers between devices, body(): lax.all_to_all(spectrum, 'gz', split_axis=3, concat_axis=4, tiled=True)  6.38 us
    all_to_all x1, starting transfers between devices, body(): lax.all_to_all(spectrum, 'gz', split_axis=3, concat_axis=4, tiled=True)  6.35 us
    add x1, other arithmetic, body(): theta_next = theta + section_gain * section_next  5.98 us
    select_n x4, other arithmetic, interpolate(): live_weight = jnp.where(taps_index < live_count, taps_weight, 0.0)  5.92 us
  transfers between devices with their start and end apart: 8, of which 5 were waited for; matrix products, arithmetic and copies ran while one was open for 61% of the time, Pallas kernels for 0%

commit v1 on v0

v1 whole, which is shorter than its diff:
```python
import functools
import math

import jax
import jax.numpy as jnp
import numpy as np
from jax import lax
from jax.experimental import pallas as pl
from jax.experimental.pallas import tpu as pltpu
from jax.sharding import PartitionSpec as P

MESH = pl.DeviceIdType.MESH
VMEM = pltpu.VMEM
LANES = 128
HALO = 4

first_coeffs = (0.8, -0.2, 4.0 / 105.0, -1.0 / 280.0)
second_coeffs = (1.6, -0.2, 8.0 / 315.0, -1.0 / 560.0)
center_coeff = -205.0 / 72.0
diffusivity = 0.15
time_step = 0.4
section_keep = -5.0 / 9.0
section_gain = 15.0 / 16.0


def whole_vmem(count):
    return [pl.BlockSpec(memory_space=VMEM)] * count


def modes_kernel(peers, spec_ref, out_ref, send, send_sem, recv_sem, own_sem):
    me = lax.axis_index("gz")
    barrier = pltpu.get_barrier_semaphore()
    for step in range(1, peers):
        pl.semaphore_signal(
            barrier, inc=1, device_id={"gz": lax.rem(me + step, peers)}, device_id_type=MESH
        )
    _, _, rows, depth, modes = spec_ref.shape
    mine = depth // peers
    lines = 3 * rows * mine
    for peer in range(peers):
        for slab in range(modes // LANES):
            for part in range(2):
                for comp in range(3):
                    for row in range(rows):
                        at = part * lines + (comp * rows + row) * mine
                        send[peer, slab, at : at + mine, :] = spec_ref[
                            comp,
                            part,
                            row,
                            peer * mine : (peer + 1) * mine,
                            slab * LANES : (slab + 1) * LANES,
                        ]
    pl.semaphore_wait(barrier, peers - 1)
    copies = []
    for step in range(1, peers):
        target = lax.rem(me + step, peers)
        copy = pltpu.make_async_remote_copy(
            src_ref=send.at[target],
            dst_ref=out_ref.at[me],
            send_sem=send_sem.at[step - 1],
            recv_sem=recv_sem.at[step - 1],
            device_id={"gz": target},
            device_id_type=MESH,
        )
        copy.start()
        copies.append(copy)
    own = pltpu.make_async_copy(send.at[me], out_ref.at[me], own_sem)
    own.start()
    own.wait()
    for copy in copies:
        copy.wait()


def exchange_modes(spectrum):
    peers = lax.axis_size("gz")
    _, _, rows, depth, modes = spectrum.shape
    shape = (peers, modes // LANES, 6 * rows * (depth // peers), LANES)
    return pl.pallas_call(
        functools.partial(modes_kernel, peers),
        out_shape=jax.ShapeDtypeStruct(shape, jnp.float32),
        in_specs=whole_vmem(1),
        out_specs=pl.BlockSpec(memory_space=VMEM),
        scratch_shapes=[
            VMEM(shape, jnp.float32),
            pltpu.SemaphoreType.DMA((peers - 1,)),
            pltpu.SemaphoreType.DMA((peers - 1,)),
            pltpu.SemaphoreType.DMA,
        ],
        compiler_params=pltpu.CompilerParams(collective_id=0, has_side_effects=True),
        name="modes",
    )(spectrum)


def rotate(value, turn):
    re, im = value
    cosine, sine = math.cos(2 * math.pi * turn), math.sin(2 * math.pi * turn)
    quarter = turn * 4 % 4
    if quarter == 0:
        return re, im
    if quarter == 1:
        return -im, re
    if quarter == 2:
        return -re, -im
    if quarter == 3:
        return im, -re
    return re * cosine - im * sine, re * sine + im * cosine


def fft(values):
    count = len(values)
    if count == 1:
        return values
    even = fft(values[0::2])
    odd = fft(values[1::2])
    low, high = [], []
    for x in range(count // 2):
        re, im = rotate(odd[x], x / count)
        low.append((even[x][0] + re, even[x][1] + im))
        high.append((even[x][0] - re, even[x][1] - im))
    return low + high


def split(value):
    top = value.astype(jnp.bfloat16)
    return top, (value - top.astype(jnp.float32)).astype(jnp.bfloat16)


def lines_kernel(offset_ref, spec_ref, twist_ref, last_ref, out_ref, mixed, velocity):
    slabs, both, _ = spec_ref.shape
    lines = both // 2
    near = 2 * slabs
    group = lines // 3
    for comp in range(3):
        re_rows = slice(comp * group, (comp + 1) * group)
        im_rows = slice(lines + comp * group, lines + (comp + 1) * group)
        values = [(spec_ref[k, re_rows, :], spec_ref[k, im_rows, :]) for k in range(slabs)]
        even = fft(values)
        for x in range(slabs):
            mixed[2 * x, re_rows, :] = even[x][0]
            mixed[2 * x, im_rows, :] = even[x][1]
        values = [(spec_ref[k, re_rows, :], spec_ref[k, im_rows, :]) for k in range(slabs)]
        odd = fft([rotate(values[k], k / near) for k in range(slabs)])
        for x in range(slabs):
            mixed[2 * x + 1, re_rows, :] = odd[x][0]
            mixed[2 * x + 1, im_rows, :] = odd[x][1]
    last_both = last_ref[...]
    far = last_both.shape[0] // 2
    last_top = last_both[:far]
    dims = (((1,), (1,)), ((), ()))

    def twisted(line):
        re, im = mixed[:, line, :], mixed[:, lines + line, :]
        pieces = []
        for quarter in range(LANES // near):
            rows = slice(quarter * near, (quarter + 1) * near)
            cosine, sine = twist_ref[0, rows, :], twist_ref[1, rows, :]
            pieces.append(jnp.concatenate([re * cosine - im * sine, re * sine + im * cosine], axis=1))
        return jnp.concatenate(pieces, axis=0)

    for pair in range(lines // 2):
        turned = jnp.concatenate([twisted(2 * pair), twisted(2 * pair + 1)], axis=0)
        top, rest = split(turned)
        first = lax.dot_general(last_both, top, dims, preferred_element_type=jnp.float32)
        second = lax.dot_general(last_top, rest, dims, preferred_element_type=jnp.float32)
        total = first[:far] + (first[far:] + second)
        velocity[:, 2 * pair, :] = total[:, :LANES]
        velocity[:, 2 * pair + 1, :] = total[:, LANES:]
    blocks, span = out_ref.shape[:2]
    for block in range(blocks):
        start = jnp.minimum(offset_ref[block] // LANES, far - span)
        out_ref[block] = velocity[pl.ds(start, span)]


def transform_lines(seg_offset, modes):
    blocks = seg_offset.shape[0]
    slabs, both, _ = modes.shape
    lines = both // 2
    length = 2 * slabs * LANES
    far = length // LANES
    span = min(3 * length // (2 * blocks) // LANES + 1, far)
    k = np.arange(LANES)
    turn = 2 * np.pi * (np.outer(k, k) % length) / length
    twist = np.stack([np.cos(turn), np.sin(turn)]).astype(np.float32)
    turn = 2 * np.pi * (np.outer(np.arange(far), k) % far) / far
    last = np.concatenate([np.cos(turn), -np.sin(turn)], axis=1).astype(np.float32)
    top = last.astype(jnp.bfloat16)
    rest = (last - top.astype(np.float32)).astype(jnp.bfloat16)
    return pl.pallas_call(
        lines_kernel,
        out_shape=jax.ShapeDtypeStruct((blocks, span, lines, LANES), jnp.float32),
        in_specs=[pl.BlockSpec(memory_space=pltpu.SMEM)] + whole_vmem(3),
        out_specs=pl.BlockSpec(memory_space=VMEM),
        scratch_shapes=[
            VMEM((2 * slabs, both, LANES), jnp.float32),
            VMEM((far, lines, LANES), jnp.float32),
        ],
        name="lines",
    )(seg_offset, modes, jnp.asarray(twist), jnp.asarray(np.concatenate([top, rest], axis=0)))


def faces_kernel(sizes, seg_ref, theta_ref, *refs):
    out_ref, halos = refs[0], refs[1:7]
    send_sem, recv_sem, own_sem = refs[7:]
    gx, gy, gz = sizes
    me = lax.axis_index("gx")
    rows, depth, cells = theta_ref.shape
    barrier = pltpu.get_barrier_semaphore()
    targets = [{"gx": lax.rem(me + step, gx)} for step in range(1, gx)]
    for axis, count in (("gy", gy), ("gz", gz)):
        here = lax.axis_index(axis)
        targets.append({axis: lax.rem(here + 1, count)})
        targets.append({axis: lax.rem(here + count - 1, count)})
    for target in targets:
        pl.semaphore_signal(barrier, inc=1, device_id=target, device_id_type=MESH)
    pl.semaphore_wait(barrier, len(targets))
    sends = []
    for step in range(1, gx):
        target = lax.rem(me + step, gx)
        sends.append((seg_ref.at[target], out_ref.at[me], {"gx": target}))
    ahead = {
        axis: {axis: lax.rem(lax.axis_index(axis) + 1, count)}
        for axis, count in (("gx", gx), ("gy", gy), ("gz", gz))
    }
    behind = {
        axis: {axis: lax.rem(lax.axis_index(axis) + count - 1, count)}
        for axis, count in (("gx", gx), ("gy", gy), ("gz", gz))
    }
    x_back, x_front, y_back, y_front, z_back, z_front = halos
    sends += [
        (theta_ref.at[:, pl.ds(depth - HALO, HALO), :], z_back, ahead["gz"]),
        (theta_ref.at[:, pl.ds(0, HALO), :], z_front, behind["gz"]),
        (theta_ref.at[:, :, pl.ds(cells - LANES, LANES)], x_back, ahead["gx"]),
        (theta_ref.at[:, :, pl.ds(0, LANES)], x_front, behind["gx"]),
        (theta_ref.at[pl.ds(rows - HALO, HALO)], y_back, ahead["gy"]),
        (theta_ref.at[pl.ds(0, HALO)], y_front, behind["gy"]),
    ]
    copies = []
    for number, (source, place, device) in enumerate(sends):
        copy = pltpu.make_async_remote_copy(
            src_ref=source,
            dst_ref=place,
            send_sem=send_sem.at[number],
            recv_sem=recv_sem.at[number],
            device_id=device,
            device_id_type=MESH,
        )
        copy.start()
        copies.append(copy)
    own = pltpu.make_async_copy(seg_ref.at[me], out_ref.at[me], own_sem)
    own.start()
    own.wait()
    for copy in copies:
        copy.wait()


def exchange_faces(segments, theta):
    sizes = tuple(lax.axis_size(axis) for axis in ("gx", "gy", "gz"))
    rows, depth, cells = theta.shape
    shapes = [
        segments.shape,
        (rows, depth, LANES),
        (rows, depth, LANES),
        (HALO, depth, cells),
        (HALO, depth, cells),
        (rows, HALO, cells),
        (rows, HALO, cells),
    ]
    count = sizes[0] - 1 + 6
    return pl.pallas_call(
        functools.partial(faces_kernel, sizes),
        out_shape=[jax.ShapeDtypeStruct(shape, jnp.float32) for shape in shapes],
        in_specs=whole_vmem(2),
        out_specs=whole_vmem(7),
        scratch_shapes=[
            pltpu.SemaphoreType.DMA((count,)),
            pltpu.SemaphoreType.DMA((count,)),
            pltpu.SemaphoreType.DMA,
        ],
        compiler_params=pltpu.CompilerParams(collective_id=1, has_side_effects=True),
        name="faces",
    )(segments, theta)


CHUNK = 256


def section_kernel(
    offset_ref, length_ref, seg_ref, x_back, x_front, y_back, y_front, z_back, z_front,
    theta_ref, sum_ref, index_ref, weight_ref, theta_out, sum_out,
    gathered, pieces, carried, deep, position, top_weight, rest_weight,
):
    me = lax.axis_index("gx")
    rows, depth, cells = theta_ref.shape
    blocks, span, lines, _ = seg_ref.shape
    taps = index_ref.shape[0]
    total = blocks * lines
    for block in range(blocks):
        gathered[0:span, block * lines : (block + 1) * lines, :] = seg_ref[block]
    top, rest = split(gathered[0:span])
    pieces[0:span, 0:total, :] = top
    pieces[0:span, total:, :] = rest
    pieces[span] = jnp.zeros(pieces.shape[1:], pieces.dtype)

    columns = pl.ds(pl.multiple_of(me * cells, LANES), cells)
    index = index_ref[:, columns]
    weight = jnp.where(index < length_ref[me], weight_ref[:, columns], 0.0)
    live = index < length_ref[me]
    merged = jnp.zeros_like(weight)
    for tap in range(taps):
        merged = merged + jnp.where(index == index[tap : tap + 1], weight[tap : tap + 1], 0.0)
    high, low = split(merged)
    top_weight[...] = high.astype(jnp.float32)
    rest_weight[...] = low.astype(jnp.float32)
    begin = offset_ref[me] - length_ref[blocks + me] * LANES
    place = index + begin
    position[...] = jnp.where(live, place, -1)
    bounds = []
    for chunk in range(cells // CHUNK):
        part = slice(chunk * CHUNK, (chunk + 1) * CHUNK)
        seen = live[:, part]
        least = jnp.min(jnp.where(seen, place[:, part], span * LANES))
        most = jnp.max(jnp.where(seen, place[:, part], -1))
        bounds.append((least // LANES, (most + LANES) // LANES))

    counter = lax.broadcasted_iota(jnp.int32, (2 * LANES, CHUNK), 0).astype(jnp.float32).astype(jnp.bfloat16)
    for chunk in range(cells // CHUNK):
        part = slice(chunk * CHUNK, (chunk + 1) * CHUNK)
        least, end = bounds[chunk]

        def tile(step, acc):
            slab = least + 2 * step
            near = position[:, part] - slab * LANES
            near = jnp.clip(near, -1, 2 * LANES).astype(jnp.float32)
            near = near.astype(jnp.bfloat16)
            tops = top_weight[:, part].astype(jnp.bfloat16)
            rests = rest_weight[:, part].astype(jnp.bfloat16)
            matrix_top = jnp.zeros((2 * LANES, CHUNK), jnp.bfloat16)
            matrix_rest = jnp.zeros((2 * LANES, CHUNK), jnp.bfloat16)
            for tap in range(taps):
                hit = counter == near[tap : tap + 1]
                matrix_top = jnp.where(hit, tops[tap : tap + 1], matrix_top)
                matrix_rest = jnp.where(hit, rests[tap : tap + 1], matrix_rest)
            values = jnp.concatenate([pieces[slab], pieces[slab + 1]], axis=1)
            first = jnp.dot(values, matrix_top, preferred_element_type=jnp.float32)
            second = jnp.dot(values[:total], matrix_rest, preferred_element_type=jnp.float32)
            return acc + (first[:total] + (first[total:] + second))

        result = lax.fori_loop(
            0, (end - least + 1) // 2, tile, jnp.zeros((total, CHUNK), jnp.float32)
        )
        own = lines // (3 * depth)
        for block in range(blocks):
            for comp in range(3):
                for row in range(own):
                    at = block * lines + (comp * own + row) * depth
                    carried[comp, block * own + row, :, part] = result[at : at + depth]

    deep[:, 0:HALO, :] = z_back[...]
    deep[:, HALO : HALO + depth, :] = theta_ref[...]
    deep[:, HALO + depth :, :] = z_front[...]

    def line(row):
        if row < 0:
            return y_back[HALO + row]
        if row >= rows:
            return y_front[row - rows]
        return theta_ref[row]

    for row in range(rows):
        center = theta_ref[row]
        wide = jnp.concatenate([x_back[row], center, x_front[row]], axis=1)
        width = wide.shape[1]
        grads = [None, None, None]
        laplace = 3.0 * center_coeff * center
        for reach in range(1, 5):
            pairs = [
                (
                    pltpu.roll(wide, width - reach, 1)[:, LANES : LANES + cells],
                    pltpu.roll(wide, reach, 1)[:, LANES : LANES + cells],
                ),
                (line(row + reach), line(row - reach)),
                (deep[row, HALO + reach : HALO + reach + depth], deep[row, HALO - reach : HALO - reach + depth]),
            ]
            joined = None
            for axis, (ahead, behind) in enumerate(pairs):
                term = first_coeffs[reach - 1] * (ahead - behind)
                grads[axis] = term if grads[axis] is None else grads[axis] + term
                both = ahead + behind
                joined = both if joined is None else joined + both
            laplace = laplace + second_coeffs[reach - 1] * joined
        moved = carried[0, row] * grads[0] + carried[1, row] * grads[1] + carried[2, row] * grads[2]
        change = diffusivity * laplace - moved
        after = section_keep * sum_ref[row] + time_step * change
        sum_out[row] = after
        theta_out[row] = center + section_gain * after


def finish(seg_offset, seg_table, segments, halos, theta, section_sum, stencil_index, stencil_weight):
    blocks, span, lines, _ = segments.shape
    rows, depth, cells = theta.shape
    taps = stencil_index.shape[0]
    return pl.pallas_call(
        section_kernel,
        out_shape=[jax.ShapeDtypeStruct(theta.shape, jnp.float32)] * 2,
        in_specs=[pl.BlockSpec(memory_space=pltpu.SMEM)] * 2 + whole_vmem(11),
        out_specs=whole_vmem(2),
        scratch_shapes=[
            VMEM((span, blocks * lines, LANES), jnp.float32),
            VMEM((span + 1, 2 * blocks * lines, LANES), jnp.bfloat16),
            VMEM((3, rows, depth, cells), jnp.float32),
            VMEM((rows, depth + 2 * HALO, cells), jnp.float32),
            VMEM((taps, cells), jnp.int32),
            VMEM((taps, cells), jnp.float32),
            VMEM((taps, cells), jnp.float32),
        ],
        name="section",
    )(seg_offset, seg_table, segments, *halos, theta, section_sum, stencil_index, stencil_weight)


def body(spectrum, theta, section_sum, seg_offset, seg_length, stencil_index, stencil_weight):
    modes = exchange_modes(spectrum)
    modes = modes.reshape((-1,) + modes.shape[2:])
    segments = transform_lines(seg_offset, modes)
    segments, *halos = exchange_faces(segments, theta)
    far = 2 * modes.shape[0]
    start = jnp.minimum(seg_offset // LANES, far - segments.shape[1])
    return tuple(
        finish(
            seg_offset, jnp.concatenate([seg_length, start]), segments, halos, theta, section_sum,
            stencil_index, stencil_weight,
        )
    )


def solution(mesh):
    placed = (
        P(None, None, ("gy", "gx"), None, "gz"),
        P("gy", "gz", "gx"),
        P("gy", "gz", "gx"),
        P(),
        P(),
        P(),
        P(),
    )
    return jax.shard_map(
        body,
        mesh=mesh,
        in_specs=placed,
        out_specs=(P("gy", "gz", "gx"), P("gy", "gz", "gx")),
        check_vma=False,
    )
```

time: 178 us -> 48.5 us (0.27)
  matrix products: 90.1 us -> 0 us
  Pallas kernels: 0 us -> 46.2 us
  waiting for transfers between devices: 34.2 us -> 0 us
  other arithmetic: 18.5 us -> 0.66 us
  starting transfers between devices: 15.1 us -> 0 us
  loops' own time: 10.3 us -> 0 us
  local copies, waits for them, and re-layouts: 8.11 us -> 1.29 us
    dot_general x10 -> x0, matrix products: 90.1 us -> none  [contract(): jnp.einsum(pattern, first_term, second_term, precision=lax.Precision.HIGH...]
    pallas_call x0 -> x4, Pallas kernels: none -> 46.2 us  [the longest x1 19.3 us: exchange_faces(): pl.pallas_call(functools.partial(faces_kernel, sizes), out_shape=[jax.Sha...]
    ppermute x6 -> x0, waiting for transfers between devices: 20.5 us -> none  [the longest x3 17.4 us: extended(): lax.ppermute(head, axis, [((i + 1) % count, i) for i in range(count)])]
    all_to_all x2 -> x0, waiting for transfers between devices: 13.7 us -> none  [the longest x1 7.29 us: body(): lax.all_to_all(pieces, 'gx', split_axis=0, concat_axis=2, tiled=True)[0]]
    another operation x1 -> x0, loops' own time: 10.3 us -> none  [body(): pieces = lax.map(sample, block_numbers)]
    all_to_all x2 -> x0, starting transfers between devices: 10.1 us -> none  [the longest x1 6.35 us: body(): lax.all_to_all(spectrum, 'gz', split_axis=3, concat_axis=4, tiled=True)]
    add x1 -> x0, other arithmetic: 5.98 us -> none  [body(): theta_next = theta + section_gain * section_next]
    select_n x4 -> x0, other arithmetic: 5.92 us -> none  [interpolate(): live_weight = jnp.where(taps_index < live_count, taps_weight, 0.0)]
  transfers between devices with their start and end apart: 8 -> 0, of which waited for: 5 -> 0; matrix products, arithmetic and copies ran while one was open for 61% -> 0% of each run, Pallas kernels for 0% -> 0%
where the time goes in v1:
time: 48.5 us; the launch traced here: 48.8 us
  Pallas kernels  46.2 us (95%)
  local copies, waits for them, and re-layouts  1.29 us (3%)
  other arithmetic  0.66 us (1%)
  between operations  0.66 us (1%)
    pallas_call x1, Pallas kernels, exchange_faces(): pl.pallas_call(functools.partial(faces_kernel, sizes), out_shape=[jax.Sha...  19.3 us
    pallas_call x1, Pallas kernels, exchange_modes(): pl.pallas_call(functools.partial(modes_kernel, peers), out_shape=jax.Shap...  14.2 us
    pallas_call x1, Pallas kernels, finish(): pl.pallas_call(section_kernel, out_shape=[jax.ShapeDtypeStruct(theta.shap...  9.04 us
    pallas_call x1, Pallas kernels, transform_lines(): pl.pallas_call(lines_kernel, out_shape=jax.ShapeDtypeStruct((blocks, span...  3.69 us
    unnamed x4, local copies, waits for them, and re-layouts  1.29 us

profile of v1, /device:TPU:0, one launch (start us, length us, event | category | flops | bytes accessed | tf_op | source)
XLA Modules:
  0.0 48.8 jit_solution(3796997394235563811)
XLA Ops:
  0.6 14.2 %modes.1 = f32[4,4,48,128]{3,2,1,0:T(8,128)} custom-call(f32[3,2,2,16,512]{4,3,2,1,0:T(8,128)} %spec_ref.1), custom_call_target="tpu_custom_call" | custom-call | tf_op jit(solution)/shard_map/modes/pallas_call | solution.py:78
  14.8 3.7 %lines.1.seg_ref = f32[4,13,24,128]{3,2,1,0:T(8,128)} custom-call(s32[4]{0:T(128)} %offset_ref.3, f32[16,48,128]{2,1,0:T(8,128)} %bitcast.1, f32[2,128,128]{2,1,0:T(8,128)} %constant.22.clone.twist_ref, bf16[64,256]{1,0:T(8,128)(2,1)} %constant.23.clone.last_ref), custom_call_target="tpu_custom_call" | custom-call | tf_op jit(solution)/shard_map/lines/pallas_call | solution.py:188
  18.5 19.3 %faces.1 = (f32[4,13,24,128]{3,2,1,0:T(8,128)}, f32[8,4,128]{2,1,0:T(4,128)}, f32[8,4,128]{2,1,0:T(4,128)}, f32[4,4,2048]{2,1,0:T(4,128)}, f32[4,4,2048]{2,1,0:T...) custom-call(f32[4,13,24,128]{3,2,1,0:T(8,128)} %lines.1.seg_ref, f32[8,4,2048]{2,1,0:T(4,128)} %theta_ref.3), custom_call_target="tpu_custom_call" | custom-call | tf_op jit(solution)/shard_map/faces/pallas_call | solution.py:269
  37.8 0.0 copy-start
  37.8 0.6 %copy-done = s32[4]{0:T(128)S(1)} copy-done((s32[4]{0:T(128)S(1)}, s32[4]{0:T(128)}, u32[]{:S(2)}) %copy-start) | copy-done | bytes 40
  38.5 0.0 copy-start.1
  38.5 0.6 %copy-done.1 = s32[4]{0:T(128)S(1)} copy-done((s32[4]{0:T(128)S(1)}, s32[4]{0:T(128)}, u32[]{:S(2)}) %copy-start.1) | copy-done | bytes 40
  39.1 0.6 %pad_add_fusion.length_ref = s32[8]{0:T(128)} fusion(s32[4]{0:T(128)S(1)} %fusion, s32[4]{0:T(128)S(1)} %copy-done.1), kind=kLoop, calls=%fused_computation.4 | loop fusion | flops 8 | bytes 64 | tf_op jit(solution)/shard_map/concatenate | solution.py:429
  39.8 9.0 %section.1 = (f32[8,4,2048]{2,1,0:T(4,128)}, f32[8,4,2048]{2,1,0:T(4,128)}) custom-call(s32[4]{0:T(128)} %offset_ref.3, s32[8]{0:T(128)} %pad_add_fusion.length_ref, f32[4,13,24,128]{3,2,1,0:T(8,128)} %get-tuple-element.9.seg_ref, f32[8,4,128]{2,1,0:T(4,128)} %get-tuple-element.10.x_back, f32[8,4,128]{2,1,0:T(4,128)} %get-tuple-element.11.x_front, ...), custom_call_target="tpu_custom_call" | custom-call | tf_op jit(solution)/shard_map/section/pallas_call | solution.py:402
  (1 shorter events, 0.0 us)
Async XLA Ops:
  37.8 0.7 %copy-start = (s32[4]{0:T(128)S(1)}, s32[4]{0:T(128)}, u32[]{:S(2)}) copy-start(s32[4]{0:T(128)} %offset_ref.3) | copy-start | bytes 52
  38.5 0.7 %copy-start.1 = (s32[4]{0:T(128)S(1)}, s32[4]{0:T(128)}, u32[]{:S(2)}) copy-start(s32[4]{0:T(128)} %param.13) | copy-start | bytes 52

commit v2 on v0

v2 whole, which is shorter than its diff:
```python
import functools
import math

import jax
import jax.numpy as jnp
import numpy as np
from jax import lax
from jax.experimental import pallas as pl
from jax.experimental.pallas import tpu as pltpu
from jax.sharding import PartitionSpec as P

MESH = pl.DeviceIdType.MESH
VMEM = pltpu.VMEM
LANES = 128
HALO = 4

first_coeffs = (0.8, -0.2, 4.0 / 105.0, -1.0 / 280.0)
second_coeffs = (1.6, -0.2, 8.0 / 315.0, -1.0 / 560.0)
center_coeff = -205.0 / 72.0
diffusivity = 0.15
time_step = 0.4
section_keep = -5.0 / 9.0
section_gain = 15.0 / 16.0


def whole_vmem(count):
    return [pl.BlockSpec(memory_space=VMEM)] * count


def rotate(value, turn):
    re, im = value
    cosine, sine = math.cos(2 * math.pi * turn), math.sin(2 * math.pi * turn)
    quarter = turn * 4 % 4
    if quarter == 0:
        return re, im
    if quarter == 1:
        return -im, re
    if quarter == 2:
        return -re, -im
    if quarter == 3:
        return im, -re
    return re * cosine - im * sine, re * sine + im * cosine


def fft(values):
    count = len(values)
    if count == 1:
        return values
    even = fft(values[0::2])
    odd = fft(values[1::2])
    low, high = [], []
    for x in range(count // 2):
        re, im = rotate(odd[x], x / count)
        low.append((even[x][0] + re, even[x][1] + im))
        high.append((even[x][0] - re, even[x][1] - im))
    return low + high


def split(value):
    top = value.astype(jnp.bfloat16)
    return top, (value - top.astype(jnp.float32)).astype(jnp.bfloat16)


def section_kernel(
    sizes, span,
    offset_ref, length_ref, spec_ref, theta_ref, sum_ref, index_ref, weight_ref, twist_ref, last_ref,
    theta_out, sum_out,
    modes_send, modes_recv, mixed, velocity, seg_send, seg_recv, matrix_top, matrix_rest, gathered, values,
    grads, laplace, deep, x_back, x_front, y_back, y_front, z_back, z_front,
    modes_sems, seg_sems, face_sems,
):
    gx, gy, gz = sizes
    here = {axis: lax.axis_index(axis) for axis in ("gx", "gy", "gz")}
    counts = dict(gx=gx, gy=gy, gz=gz)
    ahead = {axis: {axis: lax.rem(here[axis] + 1, counts[axis])} for axis in here}
    behind = {axis: {axis: lax.rem(here[axis] + counts[axis] - 1, counts[axis])} for axis in here}
    rows, depth, cells = theta_ref.shape
    _, _, own_rows, all_depth, modes = spec_ref.shape
    local_slabs = modes // LANES
    group = own_rows * depth
    slabs = gz * local_slabs
    near = 2 * slabs
    far = 2 * slabs
    taps = index_ref.shape[0]

    barrier = pltpu.get_barrier_semaphore()
    targets = [{"gx": lax.rem(here["gx"] + step, gx)} for step in range(1, gx)]
    targets += [{"gz": lax.rem(here["gz"] + step, gz)} for step in range(1, gz)]
    targets += [ahead["gy"], behind["gy"]]
    for target in targets:
        pl.semaphore_signal(barrier, inc=1, device_id=target, device_id_type=MESH)

    for comp in range(3):
        for slab in range(local_slabs):
            for part in range(2):
                for row in range(own_rows):
                    held = spec_ref[comp, part, row, :, slab * LANES : (slab + 1) * LANES]
                    at = part * group + row * depth
                    for peer in range(gz):
                        modes_send[comp, peer, slab, at : at + depth, :] = held[
                            peer * depth : (peer + 1) * depth
                        ]
    pl.semaphore_wait(barrier, len(targets))

    def modes_copy(comp, step):
        target = lax.rem(here["gz"] + step, gz)
        return pltpu.make_async_remote_copy(
            src_ref=modes_send.at[comp, target],
            dst_ref=modes_recv.at[comp, here["gz"]],
            send_sem=modes_sems.at[0, comp, step - 1],
            recv_sem=modes_sems.at[1, comp, step - 1],
            device_id={"gz": target},
            device_id_type=MESH,
        )

    def seg_copy(comp, step):
        target = lax.rem(here["gx"] + step, gx)
        return pltpu.make_async_remote_copy(
            src_ref=seg_send.at[comp, target],
            dst_ref=seg_recv.at[comp, here["gx"]],
            send_sem=seg_sems.at[0, comp, step - 1],
            recv_sem=seg_sems.at[1, comp, step - 1],
            device_id={"gx": target},
            device_id_type=MESH,
        )

    faces = [
        pltpu.make_async_remote_copy(
            src_ref=source,
            dst_ref=place,
            send_sem=face_sems.at[0, number],
            recv_sem=face_sems.at[1, number],
            device_id=device,
            device_id_type=MESH,
        )
        for number, (source, place, device) in enumerate(
            [
                (theta_ref.at[:, :, pl.ds(cells - LANES, LANES)], x_back, ahead["gx"]),
                (theta_ref.at[:, :, pl.ds(0, LANES)], x_front, behind["gx"]),
                (theta_ref.at[pl.ds(rows - HALO, HALO)], y_back, ahead["gy"]),
                (theta_ref.at[pl.ds(0, HALO)], y_front, behind["gy"]),
                (theta_ref.at[:, pl.ds(depth - HALO, HALO), :], z_back, ahead["gz"]),
                (theta_ref.at[:, pl.ds(0, HALO), :], z_front, behind["gz"]),
            ]
        )
    ]
    for comp in range(3):
        for step in range(1, gz):
            modes_copy(comp, step).start()
    for face in faces:
        face.start()
    for comp in range(3):
        modes_recv[comp, here["gz"]] = modes_send[comp, here["gz"]]

    me = here["gx"]
    live_count = length_ref[me]
    begin = offset_ref[me] - jnp.minimum(offset_ref[me] // LANES, far - span) * LANES
    counter = lax.broadcasted_iota(jnp.int32, (LANES, LANES), 0).astype(jnp.float32).astype(jnp.bfloat16)

    def spread(row):
        one = jnp.broadcast_to(row, (16, LANES)).astype(jnp.bfloat16)
        return jnp.concatenate([one] * (LANES // 16), axis=0)

    def build(chunk, carry):
        columns = pl.ds(pl.multiple_of(me * cells + chunk * LANES, LANES), LANES)
        index = index_ref[:, columns]
        live = index < live_count
        weight = jnp.where(live, weight_ref[:, columns], 0.0)
        merged = jnp.zeros_like(weight)
        for tap in range(taps):
            merged = merged + jnp.where(index == index[tap : tap + 1], weight[tap : tap + 1], 0.0)
        high, low = split(merged)
        high, low = high.astype(jnp.float32), low.astype(jnp.float32)
        place = jnp.where(live, index + begin, -1)
        tops = [spread(high[tap : tap + 1]) for tap in range(taps)]
        rests = [spread(low[tap : tap + 1]) for tap in range(taps)]

        def slab_of(slab, inner):
            close = jnp.clip(place - slab * LANES, -1, LANES).astype(jnp.float32)
            top = jnp.zeros((LANES, LANES), jnp.bfloat16)
            rest = jnp.zeros((LANES, LANES), jnp.bfloat16)
            for tap in range(taps):
                hit = counter == spread(close[tap : tap + 1])
                top = jnp.where(hit, tops[tap], top)
                rest = jnp.where(hit, rests[tap], rest)
            at = pl.ds(pl.multiple_of(slab * LANES, LANES), LANES)
            matrix_top[chunk, at, :] = top
            matrix_rest[chunk, at, :] = rest
            return inner

        return lax.fori_loop(0, span, slab_of, carry)

    lax.fori_loop(0, cells // LANES, build, 0)

    last_both = last_ref[...]
    last_top = last_both[:far]
    dims = (((1,), (1,)), ((), ()))

    def twisted(line):
        re, im = mixed[:, line, :], mixed[:, group + line, :]
        pieces = []
        for quarter in range(LANES // near):
            part = slice(quarter * near, (quarter + 1) * near)
            cosine, sine = twist_ref[0, part, :], twist_ref[1, part, :]
            pieces.append(jnp.concatenate([re * cosine - im * sine, re * sine + im * cosine], axis=1))
        return jnp.concatenate(pieces, axis=0)

    def transform(comp, carry):
        for step in range(1, gz):
            modes_copy(comp, step).wait()

        def arrived(k):
            held = modes_recv[comp, k // local_slabs, k % local_slabs]
            return held[:group], held[group:]

        for parity in range(2):
            mixes = fft([rotate(arrived(k), parity * k / near) for k in range(slabs)])
            for x in range(slabs):
                mixed[2 * x + parity, 0:group, :] = mixes[x][0]
                mixed[2 * x + parity, group:, :] = mixes[x][1]
        for pair in range(group // 2):
            turned = jnp.concatenate([twisted(2 * pair), twisted(2 * pair + 1)], axis=0)
            top, rest = split(turned)
            first = lax.dot_general(last_both, top, dims, preferred_element_type=jnp.float32)
            second = lax.dot_general(last_top, rest, dims, preferred_element_type=jnp.float32)
            total = first[:far] + (first[far:] + second)
            velocity[:, 2 * pair, :] = total[:, :LANES]
            velocity[:, 2 * pair + 1, :] = total[:, LANES:]
        for block in range(gx):
            start = jnp.minimum(offset_ref[block] // LANES, far - span)
            seg_send[comp, block] = velocity[pl.ds(start, span)]
        for step in range(1, gx):
            seg_copy(comp, step).start()
        seg_recv[comp, me] = seg_send[comp, me]
        return carry

    lax.fori_loop(0, 3, transform, 0)

    for face in faces[:4]:
        face.wait()

    def line(row):
        if row < 0:
            return y_back[HALO + row]
        if row >= rows:
            return y_front[row - rows]
        return theta_ref[row]

    for row in range(rows):
        at = slice(row * depth, (row + 1) * depth)
        center = theta_ref[row]
        wide = jnp.concatenate([x_back[row], center, x_front[row]], axis=1)
        width = wide.shape[1]
        grad_x = jnp.zeros_like(center)
        grad_y = jnp.zeros_like(center)
        partial = 3.0 * center_coeff * center
        for reach in range(1, 5):
            ahead_x = pltpu.roll(wide, width - reach, 1)[:, LANES : LANES + cells]
            behind_x = pltpu.roll(wide, reach, 1)[:, LANES : LANES + cells]
            ahead_y, behind_y = line(row + reach), line(row - reach)
            grad_x = grad_x + first_coeffs[reach - 1] * (ahead_x - behind_x)
            grad_y = grad_y + first_coeffs[reach - 1] * (ahead_y - behind_y)
            partial = partial + second_coeffs[reach - 1] * (ahead_x + behind_x + ahead_y + behind_y)
        grads[0, at, :] = grad_x
        grads[1, at, :] = grad_y
        laplace[at, :] = partial
    for face in faces[4:]:
        face.wait()
    deep[:, 0:HALO, :] = z_back[...]
    deep[:, HALO : HALO + depth, :] = theta_ref[...]
    deep[:, HALO + depth :, :] = z_front[...]
    for row in range(rows):
        at = slice(row * depth, (row + 1) * depth)
        grad_z = jnp.zeros((depth, cells), jnp.float32)
        partial = laplace[at, :]
        for reach in range(1, 5):
            ahead_z = deep[row, HALO + reach : HALO + reach + depth]
            behind_z = deep[row, HALO - reach : HALO - reach + depth]
            grad_z = grad_z + first_coeffs[reach - 1] * (ahead_z - behind_z)
            partial = partial + second_coeffs[reach - 1] * (ahead_z + behind_z)
        grads[2, at, :] = grad_z
        change = diffusivity * partial
        laplace[at, :] = section_keep * sum_ref[row] + time_step * change

    for comp in range(3):
        for step in range(1, gx):
            seg_copy(comp, step).wait()
    lines = gx * group
    for comp in range(3):
        for block in range(gx):
            at = (comp * gx + block) * group
            for slab in range(span):
                gathered[at : at + group, slab * LANES : (slab + 1) * LANES] = seg_recv[comp, block, slab]
    total = 3 * lines
    top, rest = split(gathered[...])
    values[0:total, :] = top
    values[total:, :] = rest

    def combine(pair, carry):
        top = jnp.concatenate([matrix_top[2 * pair], matrix_top[2 * pair + 1]], axis=1)
        rest = jnp.concatenate([matrix_rest[2 * pair], matrix_rest[2 * pair + 1]], axis=1)
        first = jnp.dot(values[...], top, preferred_element_type=jnp.float32)
        second = jnp.dot(values[0:total, :], rest, preferred_element_type=jnp.float32)
        moved = first[:total] + (first[total:] + second)
        columns = pl.ds(pl.multiple_of(pair * 2 * LANES, 2 * LANES), 2 * LANES)
        carried = None
        for comp in range(3):
            term = moved[comp * lines : (comp + 1) * lines] * grads[comp, :, columns]
            carried = term if carried is None else carried + term
        after = laplace[:, columns] - time_step * carried
        for row in range(rows):
            piece = after[row * depth : (row + 1) * depth]
            sum_out[row, :, columns] = piece
            theta_out[row, :, columns] = theta_ref[row, :, columns] + section_gain * piece
        return carry

    lax.fori_loop(0, cells // (2 * LANES), combine, 0)


def body(spectrum, theta, section_sum, seg_offset, seg_length, stencil_index, stencil_weight):
    sizes = tuple(lax.axis_size(axis) for axis in ("gx", "gy", "gz"))
    gx, _, gz = sizes
    _, _, own_rows, all_depth, modes = spectrum.shape
    rows, depth, cells = theta.shape
    group = own_rows * depth
    slabs = gz * modes // LANES
    length = 2 * slabs * LANES
    far = length // LANES
    span = min(3 * length // (2 * gx) // LANES + 1, far)
    k = np.arange(LANES)
    turn = 2 * np.pi * (np.outer(k, k) % length) / length
    twist = np.stack([np.cos(turn), np.sin(turn)]).astype(np.float32)
    turn = 2 * np.pi * (np.outer(np.arange(far), k) % far) / far
    last = np.concatenate([np.cos(turn), -np.sin(turn)], axis=1).astype(np.float32)
    top = last.astype(jnp.bfloat16)
    rest = (last - top.astype(np.float32)).astype(jnp.bfloat16)
    modes_shape = (3, gz, modes // LANES, 2 * group, LANES)
    seg_shape = (3, gx, span, group, LANES)
    lines = gx * group
    single = jnp.float32
    return tuple(
        pl.pallas_call(
            functools.partial(section_kernel, sizes, span),
            out_shape=[jax.ShapeDtypeStruct(theta.shape, single)] * 2,
            in_specs=[pl.BlockSpec(memory_space=pltpu.SMEM)] * 2 + whole_vmem(7),
            out_specs=whole_vmem(2),
            scratch_shapes=[
                VMEM(modes_shape, single),
                VMEM(modes_shape, single),
                VMEM((2 * slabs, 2 * group, LANES), single),
                VMEM((far, group, LANES), single),
                VMEM(seg_shape, single),
                VMEM(seg_shape, single),
                VMEM((cells // LANES, span * LANES, LANES), jnp.bfloat16),
                VMEM((cells // LANES, span * LANES, LANES), jnp.bfloat16),
                VMEM((3 * lines, span * LANES), single),
                VMEM((6 * lines, span * LANES), jnp.bfloat16),
                VMEM((3, rows * depth, cells), single),
                VMEM((rows * depth, cells), single),
                VMEM((rows, depth + 2 * HALO, cells), single),
                VMEM((rows, depth, LANES), single),
                VMEM((rows, depth, LANES), single),
                VMEM((HALO, depth, cells), single),
                VMEM((HALO, depth, cells), single),
                VMEM((rows, HALO, cells), single),
                VMEM((rows, HALO, cells), single),
                pltpu.SemaphoreType.DMA((2, 3, gz - 1)),
                pltpu.SemaphoreType.DMA((2, 3, gx - 1)),
                pltpu.SemaphoreType.DMA((2, 6)),
            ],
            compiler_params=pltpu.CompilerParams(
                collective_id=0, has_side_effects=True, vmem_limit_bytes=60 * 1024 * 1024
            ),
            name="section",
        )(
            seg_offset, seg_length, spectrum, theta, section_sum, stencil_index, stencil_weight,
            jnp.asarray(twist), jnp.asarray(np.concatenate([top, rest], axis=0)),
        )
    )


def solution(mesh):
    placed = (
        P(None, None, ("gy", "gx"), None, "gz"),
        P("gy", "gz", "gx"),
        P("gy", "gz", "gx"),
        P(),
        P(),
        P(),
        P(),
    )
    return jax.shard_map(
        body,
        mesh=mesh,
        in_specs=placed,
        out_specs=(P("gy", "gz", "gx"), P("gy", "gz", "gx")),
        check_vma=False,
    )
```

time: 178 us -> 35.4 us (0.20)
  matrix products: 90.1 us -> 0 us
  waiting for transfers between devices: 34.2 us -> 0 us
  Pallas kernels: 0 us -> 32 us
  other arithmetic: 18.5 us -> 0 us
  starting transfers between devices: 15.1 us -> 0 us
  loops' own time: 10.3 us -> 0 us
  local copies, waits for them, and re-layouts: 8.11 us -> 2.42 us
    dot_general x10 -> x0, matrix products: 90.1 us -> none  [contract(): jnp.einsum(pattern, first_term, second_term, precision=lax.Precision.HIGH...]
    pallas_call x0 -> x1, Pallas kernels: none -> 32 us  [body(): pl.pallas_call(functools.partial(section_kernel, sizes, span), out_shape=...]
    ppermute x6 -> x0, waiting for transfers between devices: 20.5 us -> none  [the longest x3 17.4 us: extended(): lax.ppermute(head, axis, [((i + 1) % count, i) for i in range(count)])]
    all_to_all x2 -> x0, waiting for transfers between devices: 13.7 us -> none  [the longest x1 7.29 us: body(): lax.all_to_all(pieces, 'gx', split_axis=0, concat_axis=2, tiled=True)[0]]
    another operation x1 -> x0, loops' own time: 10.3 us -> none  [body(): pieces = lax.map(sample, block_numbers)]
    all_to_all x2 -> x0, starting transfers between devices: 10.1 us -> none  [the longest x1 6.35 us: body(): lax.all_to_all(spectrum, 'gz', split_axis=3, concat_axis=4, tiled=True)]
    add x1 -> x0, other arithmetic: 5.98 us -> none  [body(): theta_next = theta + section_gain * section_next]
    select_n x4 -> x0, other arithmetic: 5.92 us -> none  [interpolate(): live_weight = jnp.where(taps_index < live_count, taps_weight, 0.0)]
  transfers between devices with their start and end apart: 8 -> 0, of which waited for: 5 -> 0; matrix products, arithmetic and copies ran while one was open for 61% -> 0% of each run, Pallas kernels for 0% -> 0%
where the time goes in v2:
time: 35.4 us; the launch traced here: 35 us
  Pallas kernels  32 us (90%)
  local copies, waits for them, and re-layouts  2.42 us (7%)
  between operations  0.65 us (2%)
    pallas_call x1, Pallas kernels, body(): pl.pallas_call(functools.partial(section_kernel, sizes, span), out_shape=...  32 us
    unnamed x4, local copies, waits for them, and re-layouts  2.42 us

profile of v2, /device:TPU:0, one launch (start us, length us, event | category | flops | bytes accessed | tf_op | source)
XLA Modules:
  0.0 35.0 jit_solution(8525591264445359382)
XLA Ops:
  0.6 32.0 %section.1 = (f32[8,4,2048]{2,1,0:T(4,128)}, f32[8,4,2048]{2,1,0:T(4,128)}) custom-call(s32[4]{0:T(128)} %offset_ref.1, s32[4]{0:T(128)} %length_ref.1, f32[3,2,2,16,512]{4,3,2,1,0:T(8,128)} %spec_ref.1, f32[8,4,2048]{2,1,0:T(4,128)} %theta_ref.1, f32[8,4,2048]{2,1,0:T(4,128)} %sum_ref.1, s32[8,8192]{1,0:T(8,128)} %index_ref.1, f32[8,8192]{1,0:T(8,128)} %weight_ref.1, ...), custom_call_target="tpu_custom_call" | custom-call | tf_op jit(solution)/shard_map/section/pallas_call | solution.py:342
  32.6 0.0 copy-start
  32.6 1.7 %copy.13 = f32[8,4,2048]{2,1,0:T(4,128)} copy(f32[8,4,2048]{2,1,0:T(4,128)} %get-tuple-element.4) | data formatting | bytes 524288
  34.3 0.0 copy-done
  34.3 0.7 %copy.14 = f32[8,4,2048]{2,1,0:T(4,128)} copy(f32[8,4,2048]{2,1,0:T(4,128)S(1)} %copy-done) | data formatting | bytes 524288
Async XLA Ops:
  32.6 1.7 %copy-start = (f32[8,4,2048]{2,1,0:T(4,128)S(1)}, f32[8,4,2048]{2,1,0:T(4,128)}, u32[]{:S(2)}) copy-start(f32[8,4,2048]{2,1,0:T(4,128)} %get-tuple-element.5) | copy-start | bytes 786436
